TPU v7x, 32 devices: a whole 2x2x4 slice. The times are simulated.
32 devices in a mesh: chan: 2 (over x), vis: 2 (over core), pix: 8 (over z, y).
Axes of the slice: x: 2, y: 2, z: 4, core: 2. Of those that a mesh axis runs over, the one named last changes fastest.
Arguments:
- response: bfloat16 [16384, 49152], P(('chan', 'vis'), 'pix'), parts along dimension 0, may hold values from -5 to 5
- vis_data: float32 [16384], P(('chan', 'vis')), parts along dimension 0, may hold values from -6 to 6
- baseline_of_row: int32 [8192], P('vis'), may hold values from 0 to 8191
- noise_class: int32 [8192], P('vis'), may hold values from 0 to 15
- baseline_weight: float32 [8192], replicated, may hold values from 0.25 to 4
- class_inv_var: float32 [32], P('chan'), parts along dimension 0, may hold values from 0.25 to 4
Outputs:
- sky_map: float32 [98304], P(('chan', 'pix')), parts along dimension 0
- psf: float32 [98304, 64], P(('chan', 'pix'), 'vis'), parts along dimension 0
There are 2 independent parts, one for each index of `chan`. A program takes and returns all parts, laid end to end along the dimension named above; an argument that names none is the same for every part. Nothing has to cross between parts.
Inputs may be any that keep to these rules, and one draw needn't show every extreme that they name: `baseline_of_row`: baseline index of each row.
All inputs are finite; a program needn't handle non-finite values.
Results may differ from a plain program's by a relative error of at most 0.0041.
Values may be sent and summed in bfloat16 or wider, within the bound.
No kernel may reach another device: no remote copies, remote signals or barrier semaphores. Data moves between devices by JAX's collectives and lax.ppermute only.
A program may use at most 128 MiB of HBM per device.

v0:
```python
import jax
import jax.numpy as jnp
from jax import lax
from jax.sharding import PartitionSpec as P

PANEL_DEV = 8


def shards(response, vis_data, baseline_of_row, noise_class, baseline_weight, class_inv_var):
    classes = lax.broadcasted_iota(jnp.int32, (1, class_inv_var.shape[0]), 1)
    class_weight = jnp.sum(
        jnp.where(noise_class[:, None] == classes, class_inv_var[None, :], jnp.float32(0.0)), axis=1
    )
    weight_row = jnp.take(baseline_weight, baseline_of_row) * class_weight
    own_panel = response[:, :PANEL_DEV]
    pix_rows = response.shape[1]
    piece_cols = lax.all_gather(own_panel, "pix", axis=1, tiled=True)
    operand = (weight_row[:, None] * piece_cols.astype(jnp.float32)).astype(jnp.bfloat16)
    plain_f = piece_cols.astype(jnp.float32)
    beam_part = jnp.concatenate(
        [
            lax.dot_general(
                response, operand, (((0,), (0,)), ((), ())), preferred_element_type=jnp.float32
            ),
            jnp.sum(weight_row[:, None] * plain_f * plain_f, axis=0)[None, :],
        ],
        axis=0,
    )
    weighted_vis = (weight_row * vis_data).astype(jnp.bfloat16)
    dirty_part = jnp.dot(weighted_vis, response, preferred_element_type=jnp.float32)
    norm_part = jnp.sum(weight_row[:, None] * jnp.square(response.astype(jnp.float32)), axis=0)
    col_share = beam_part.shape[1] // lax.axis_size("vis")
    beam_all, dirty_map, pixel_norm = lax.psum((beam_part, dirty_part, norm_part), "vis")
    beam_rows = lax.dynamic_slice_in_dim(beam_all, lax.axis_index("vis") * col_share, col_share, 1)
    panel_scale = beam_rows[pix_rows]
    beam_rows = beam_rows[:pix_rows]
    sky_map = dirty_map / jnp.sqrt(pixel_norm)
    psf = beam_rows / jnp.sqrt(pixel_norm[:, None] * panel_scale[None, :])
    return (sky_map, psf)


def solution(mesh):
    placed = (P(("chan", "vis"), "pix"), P(("chan", "vis")), P("vis"), P("vis"), P(), P("chan"))
    return jax.shard_map(
        shards,
        mesh=mesh,
        in_specs=placed,
        out_specs=(P(("chan", "pix")), P(("chan", "pix"), "vis")),
        check_vma=False,
    )
```

profile of v0, /device:TPU:0, one launch (start us, length us, event | category | flops | bytes accessed | tf_op | source)
XLA Modules:
  0.0 140.9 jit_solution(5494770655249392284)
XLA Ops:
  7.2 0.0 copy-start
  7.2 0.0 all-reduce.3.cloned.1.call-start
  7.2 0.7 fusion.2
  8.0 1.3 slice.9
  9.2 0.3 copy.14
  9.6 33.0 %all_gather.3 = bf16[4096,64]{0,1:T(8,128)(2,1)S(1)} all-gather(bf16[4096,8]{0,1:T(8,128)(2,1)S(1)} %copy.14), channel_id=1, replica_groups=mesh['chan'=2,'vis'=2,'pix'=8] {'pix'}, dimensions={1}, use_global_device_ids=true | all-gather | bytes 589824 | tf_op jit(solution)/shard_map/all_gather | solution.py:17
  42.6 0.0 copy-done
  42.6 23.0 %gather_fusion = f32[4096]{0:T(1024)S(1)} fusion(f32[8192]{0:T(1024)S(1)} %copy-done, s32[4096]{0:T(1024)S(1)} %fusion.2), kind=kCustom, calls=%fused_computation | custom fusion | bytes 49152 | tf_op jit(solution)/shard_map/jit(_take)/gather | solution.py:14
  65.6 0.9 select_reduce_fusion
  66.5 0.8 multiply_convert_fusion.2
  67.2 19.8 %convolution_bitcast_fusion = f32[6144,64]{0,1:T(8,128)S(1)} fusion(bf16[4096,6144]{1,0:T(8,128)(2,1)} %param.6, bf16[4096,64]{0,1:T(8,128)(2,1)S(1)} %all_gather.3, f32[4096]{0:T(1024)S(1)} %get-tuple-element.5), kind=kOutput, calls=%fused_computation.2 | convolution fusion | flops 3222011904 | bytes 52445184 | tf_op jit(solution)/shard_map/dot_general | solution.py:22
  87.1 0.2 fusion
  87.3 0.1 copy.13
  87.4 1.3 pad_maximum_fusion
  88.7 0.0 all-reduce.3.cloned.1.call-update
  88.7 19.3 %multiply_reduce_fusion = f32[6144]{0:T(1024)S(1)} fusion(bf16[4096,6144]{1,0:T(8,128)(2,1)} %param.6, f32[4096]{0:T(1024)S(1)} %get-tuple-element.5), kind=kLoop, calls=%fused_computation.1 | loop fusion | flops 100657152 | bytes 50372608 | tf_op jit(solution)/shard_map/reduce_sum | solution.py:31
  108.0 18.9 %fusion.3 = f32[1,6144]{1,0:T(1,128)S(1)} fusion(bf16[4096,1]{0,1:T(2,128)(2,1)S(1)} %reshape.26, bf16[4096,6144]{1,0:T(8,128)(2,1)} %param.6), kind=kOutput, calls=%fused_computation.17 | convolution fusion | flops 50331648 | bytes 50364416 | tf_op jit(solution)/shard_map/dot_general | solution.py:30
  126.9 3.5 %all-reduce = (f32[6144]{0:T(1024)S(1)}, f32[6144]{0:T(1024)S(1)}) all-reduce(f32[6144]{0:T(1024)S(1)} %bitcast.7, f32[6144]{0:T(1024)S(1)} %multiply_reduce_fusion), channel_id=1, replica_groups=mesh['chan'=2,'vis'=2,'pix'=8] {'vis'}, use_global_device_ids=true, to_apply=%region_1.2 | all-reduce | flops 12288 | bytes 98304 | tf_op jit(solution)/shard_map/psum | solution.py:33
  130.4 0.6 rsqrt_multiply_fusion
  131.1 0.0 all-reduce.3.cloned.1.call-done
  131.1 0.8 dynamic-slice_reduce_fusion
  131.9 2.2 %dynamic-slice_multiply_fusion = f32[6144,32]{0,1:T(8,128)} fusion(f32[6145,64]{0,1:T(8,128)} %all-reduce.3.cloned.1.call-done, s32[]{:T(128)S(6)} %select_n.21, f32[32]{0:T(128)S(1)} %dynamic-slice_reduce_fusion, f32[6144]{0:T(1024)S(1)} %get-tuple-element.3), kind=kLoop, calls=%fused_computation.7 | loop fusion | flops 393216 | bytes 1597572 | tf_op jit(solution)/shard_map/div | solution.py:38
  (1 shorter events, 0.0 us)
Async XLA Ops:
  7.2 35.4 %copy-start = (f32[8192]{0:T(1024)S(1)}, f32[8192]{0:T(1024)}, u32[]{:S(2)}) copy-start(f32[8192]{0:T(1024)} %param.10) | copy-start | bytes 98308
  7.2 123.9 %all-reduce.3.cloned.1.call-start = ((), (), s32[]{:S(2)}) async-start(), calls=%async_computation | async-start | bytes 3211264 | tf_op jit(solution)/shard_map/psum | solution.py:33
Sparse Core Ops, SparseCore 0:
  88.8 21.5 all-reduce.2
where the time goes:
time: 142 us; the launch traced here: 141 us
  matrix products  38.7 us (27%)
  blocking collectives  36.6 us (26%)
  other arithmetic  26 us (18%)
  local copies, waits for them, and re-layouts  25.6 us (18%)
  between operations  14.1 us (10%)
    all_gather x1, blocking collectives, shards(): piece_cols = lax.all_gather(own_panel, 'pix', axis=1, tiled=True)  33 us
    gather x1, local copies, waits for them, and re-layouts, shards(): weight_row = jnp.take(baseline_weight, baseline_of_row) * class_weight  23 us
    dot_general x1, matrix products, shards(): lax.dot_general(response, operand, (((0,), (0,)), ((), ())), preferred_el...  19.8 us
    reduce_sum x1, other arithmetic, shards(): jnp.sum(weight_row[:, None] * jnp.square(response.astype(jnp.float32)), a...  19.3 us
    dot_general x1, matrix products, shards(): jnp.dot(weighted_vis, response, preferred_element_type=jnp.float32)  18.9 us
    psum x1, blocking collectives, shards(): lax.psum((beam_part, dirty_part, norm_part), 'vis')  3.53 us
  transfers between devices with their start and end apart: 1, of which 0 were waited for; matrix products, arithmetic and copies ran while one was open for 28% of the time, Pallas kernels for 0%

commit v1 on v0

--- a/solution.py
+++ b/solution.py
@@ -14,7 +14,14 @@
     weight_row = jnp.take(baseline_weight, baseline_of_row) * class_weight
     own_panel = response[:, :PANEL_DEV]
     pix_rows = response.shape[1]
-    piece_cols = lax.all_gather(own_panel, "pix", axis=1, tiled=True)
+    size = lax.axis_size("pix")
+    right = [(i, (i + 1) % size) for i in range(size)]
+    pieces = [own_panel]
+    for far in range(1, size):
+        pieces = [lax.ppermute(pieces[0], "pix", right), *pieces]
+    full = jnp.concatenate(pieces, axis=1)
+    offset = (lax.axis_index("pix") + 1) * pieces[-1].shape[1]
+    piece_cols = jnp.roll(full, offset, axis=1)
     operand = (weight_row[:, None] * piece_cols.astype(jnp.float32)).astype(jnp.bfloat16)
     plain_f = piece_cols.astype(jnp.float32)
     beam_part = jnp.concatenate(

time: 142 us -> 144 us (1.014)
  blocking collectives: 36.6 us -> 3.57 us
  waiting for transfers between devices: 0.02 us -> 31.9 us
  starting transfers between devices: 0.04 us -> 3.14 us
    all_gather x1 -> x0, blocking collectives: 33 us -> none  [shards(): piece_cols = lax.all_gather(own_panel, 'pix', axis=1, tiled=True)]
    ppermute x0 -> x7, waiting for transfers between devices: none -> 31.8 us  [shards(): pieces = [lax.ppermute(pieces[0], 'pix', right), *pieces]]
    ppermute x0 -> x7, starting transfers between devices: none -> 3.1 us  [shards(): pieces = [lax.ppermute(pieces[0], 'pix', right), *pieces]]
  transfers between devices with their start and end apart: 1 -> 8, of which waited for: 0 -> 5; matrix products, arithmetic and copies ran while one was open for 28% -> 45% of each run, Pallas kernels for 0% -> 0%
where the time goes in v1:
time: 144 us
  matrix products  39.3 us (27%)
  waiting for transfers between devices  31.9 us (22%)
  other arithmetic  26 us (18%)
  local copies, waits for them, and re-layouts  25.7 us (18%)
  between operations  14.3 us (10%)
  blocking collectives  3.57 us (2%)
  starting transfers between devices  3.14 us (2%)
    ppermute x7, waiting for transfers between devices, shards(): pieces = [lax.ppermute(pieces[0], 'pix', right), *pieces]  31.8 us
    gather x1, local copies, waits for them, and re-layouts, shards(): weight_row = jnp.take(baseline_weight, baseline_of_row) * class_weight  23 us
    dot_general x1, matrix products, shards(): lax.dot_general(response, operand, (((0,), (0,)), ((), ())), preferred_el...  19.8 us
    dot_general x1, matrix products, shards(): jnp.dot(weighted_vis, response, preferred_element_type=jnp.float32)  19.5 us
    reduce_sum x1, other arithmetic, shards(): jnp.sum(weight_row[:, None] * jnp.square(response.astype(jnp.float32)), a...  19.3 us
    psum x1, blocking collectives, shards(): lax.psum((beam_part, dirty_part, norm_part), 'vis')  3.57 us
    ppermute x7, starting transfers between devices, shards(): pieces = [lax.ppermute(pieces[0], 'pix', right), *pieces]  3.1 us
  transfers between devices with their start and end apart: 8, of which 5 were waited for; matrix products, arithmetic and copies ran while one was open for 45% of the time, Pallas kernels for 0%

profile of v1, /device:TPU:0, one launch (start us, length us, event | category | flops | bytes accessed | tf_op | source)
XLA Modules:
  0.0 143.8 jit_solution(15782780012321286393)
XLA Ops:
  7.2 0.0 all-reduce.3.cloned.1.call-start
  7.2 1.3 slice.9
  8.5 0.3 copy.14
  8.8 3.0 %collective-permute-start = (bf16[4096,8]{0,1:T(8,128)(2,1)S(1)}, bf16[4096,8]{0,1:T(8,128)(2,1)S(1)}, u32[]{:S(2)}, u32[]{:S(2)}) collective-permute-start(bf16[4096,8]{0,1:T(8,128)(2,1)S(1)} %copy.14), channel_id=1, source_target_pairs={{0,1},{1,2},{2,3},{3,4},{4,5},{5,6},{6,7},{7,0},{8,9},{9,10},{10,1... | collective-permute-start | bytes 196616 | tf_op jit(solution)/shard_map/ppermute | solution.py:21
  11.9 5.3 %collective-permute-done = bf16[4096,8]{0,1:T(8,128)(2,1)S(1)} collective-permute-done((bf16[4096,8]{0,1:T(8,128)(2,1)S(1)}, bf16[4096,8]{0,1:T(8,128)(2,1)S(1)}, u32[]{:S(2)}, u32[]{:S(2)}) %collective-permute-start) | collective-permute-done | bytes 65568 | tf_op jit(solution)/shard_map/ppermute | solution.py:21
  17.1 7.0 %collective-permute-done.1 = bf16[4096,8]{0,1:T(8,128)(2,1)S(1)} collective-permute-done((bf16[4096,8]{0,1:T(8,128)(2,1)S(1)}, bf16[4096,8]{0,1:T(8,128)(2,1)S(1)}, u32[]{:S(2)}, u32[]{:S(2)}) %collective-permute-start.1) | collective-permute-done | bytes 65568 | tf_op jit(solution)/shard_map/ppermute | solution.py:21
  24.1 7.0 %collective-permute-done.2 = bf16[4096,8]{0,1:T(8,128)(2,1)S(1)} collective-permute-done((bf16[4096,8]{0,1:T(8,128)(2,1)S(1)}, bf16[4096,8]{0,1:T(8,128)(2,1)S(1)}, u32[]{:S(2)}, u32[]{:S(2)}) %collective-permute-start.2) | collective-permute-done | bytes 65568 | tf_op jit(solution)/shard_map/ppermute | solution.py:21
  31.1 0.7 fusion.3
  31.8 23.0 %gather_fusion = f32[4096]{0:T(1024)S(1)} fusion(f32[8192]{0:T(1024)S(1)} %copy-done, s32[4096]{0:T(1024)S(1)} %fusion.3), kind=kCustom, calls=%fused_computation | custom fusion | bytes 49152 | tf_op jit(solution)/shard_map/jit(_take)/gather | solution.py:14
  54.8 0.1 collective-permute-start.4
  54.9 0.9 select_reduce_fusion
  55.8 6.1 %collective-permute-done.4 = bf16[4096,8]{0,1:T(8,128)(2,1)S(1)} collective-permute-done((bf16[4096,8]{0,1:T(8,128)(2,1)S(1)}, bf16[4096,8]{0,1:T(8,128)(2,1)S(1)}, u32[]{:S(2)}, u32[]{:S(2)}) %collective-permute-start.4) | collective-permute-done | bytes 65568 | tf_op jit(solution)/shard_map/ppermute | solution.py:21
  61.9 0.7 multiply_convert_fusion.2
  62.6 6.6 %collective-permute-done.5 = bf16[4096,8]{0,1:T(8,128)(2,1)S(1)} collective-permute-done((bf16[4096,8]{0,1:T(8,128)(2,1)S(1)}, bf16[4096,8]{0,1:T(8,128)(2,1)S(1)}, u32[]{:S(2)}, u32[]{:S(2)}) %collective-permute-start.5) | collective-permute-done | bytes 65568 | tf_op jit(solution)/shard_map/ppermute | solution.py:21
  69.2 19.3 %multiply_reduce_fusion = f32[6144]{0:T(1024)S(1)} fusion(bf16[4096,6144]{1,0:T(8,128)(2,1)} %param.6, f32[4096]{0:T(1024)S(1)} %get-tuple-element.5), kind=kLoop, calls=%fused_computation.1 | loop fusion | flops 100657152 | bytes 50372608 | tf_op jit(solution)/shard_map/reduce_sum | solution.py:38
  88.7 19.8 %convolution_bitcast_fusion = f32[6144,64]{0,1:T(8,128)S(1)} fusion(bf16[4096,6144]{1,0:T(8,128)(2,1)} %param.6, f32[4096]{0:T(1024)S(1)} %get-tuple-element.5, bf16[4096,128]{0,1:T(8,128)(2,1)S(1)} %constant_dynamic-update-slice_fusion, s32[]{:T(128)S(6)} %select_n.35), kind=kOutput, calls=%fused_computation.2 | convolution fusion | flops 3222011904 | bytes 52445188 | tf_op jit(solution)/shard_map/dot_general | solution.py:29
  108.6 0.3 fusion
  108.8 0.1 copy.13
  108.9 1.3 pad_maximum_fusion
  110.2 19.5 %fusion.5 = f32[1,6144]{1,0:T(1,128)S(1)} fusion(bf16[4096,1]{0,1:T(2,128)(2,1)S(1)} %reshape.26, bf16[4096,6144]{1,0:T(8,128)(2,1)} %param.6), kind=kOutput, calls=%fused_computation.35 | convolution fusion | flops 50331648 | bytes 50364416 | tf_op jit(solution)/shard_map/dot_general | solution.py:37
  129.7 3.6 %all-reduce = (f32[6144]{0:T(1024)S(1)}, f32[6144]{0:T(1024)S(1)}) all-reduce(f32[6144]{0:T(1024)S(1)} %bitcast.7, f32[6144]{0:T(1024)S(1)} %multiply_reduce_fusion), channel_id=1, replica_groups=mesh['chan'=2,'vis'=2,'pix'=8] {'vis'}, use_global_device_ids=true, to_apply=%region_1.2 | all-reduce | flops 12288 | bytes 98304 | tf_op jit(solution)/shard_map/psum | solution.py:40
  133.3 0.6 rsqrt_multiply_fusion
  133.9 0.8 dynamic-slice_reduce_fusion
  134.8 2.2 %dynamic-slice_multiply_fusion = f32[6144,32]{0,1:T(8,128)} fusion(f32[6145,64]{0,1:T(8,128)} %all-reduce.3.cloned.1.call-done, s32[]{:T(128)S(6)} %select_n.36, f32[32]{0:T(128)S(1)} %dynamic-slice_reduce_fusion, f32[6144]{0:T(1024)S(1)} %get-tuple-element.3), kind=kLoop, calls=%fused_computation.7 | loop fusion | flops 393216 | bytes 1597572 | tf_op jit(solution)/shard_map/div | solution.py:45
  (28 shorter events, 0.2 us)
Async XLA Ops:
  7.2 24.6 %copy-start = (f32[8192]{0:T(1024)S(1)}, f32[8192]{0:T(1024)}, u32[]{:S(2)}) copy-start(f32[8192]{0:T(1024)} %param.10) | copy-start | bytes 98308
  7.2 126.7 %all-reduce.3.cloned.1.call-start = ((), (), s32[]{:S(2)}) async-start(), calls=%async_computation | async-start | bytes 3211264 | tf_op jit(solution)/shard_map/psum | solution.py:40
  8.8 8.3 %collective-permute-start = (bf16[4096,8]{0,1:T(8,128)(2,1)S(1)}, bf16[4096,8]{0,1:T(8,128)(2,1)S(1)}, u32[]{:S(2)}, u32[]{:S(2)}) collective-permute-start(bf16[4096,8]{0,1:T(8,128)(2,1)S(1)} %copy.14), channel_id=1, source_target_pairs={{0,1},{1,2},{2,3},{3,4},{4,5},{5,6},{6,7},{7,0},{8,9},{9,10},{10,1... | collective-permute-start | bytes 196616 | tf_op jit(solution)/shard_map/ppermute | solution.py:21
  17.1 7.0 %collective-permute-start.1 = (bf16[4096,8]{0,1:T(8,128)(2,1)S(1)}, bf16[4096,8]{0,1:T(8,128)(2,1)S(1)}, u32[]{:S(2)}, u32[]{:S(2)}) collective-permute-start(bf16[4096,8]{0,1:T(8,128)(2,1)S(1)} %collective-permute-done), channel_id=1, source_target_pairs={{0,1},{1,2},{2,3},{3,4},{4,5},{5,6},{6,7},{7,0},{8,9},{9,10},{10,1... | collective-permute-start | bytes 196616 | tf_op jit(solution)/shard_map/ppermute | solution.py:21
  24.1 7.0 %collective-permute-start.2 = (bf16[4096,8]{0,1:T(8,128)(2,1)S(1)}, bf16[4096,8]{0,1:T(8,128)(2,1)S(1)}, u32[]{:S(2)}, u32[]{:S(2)}) collective-permute-start(bf16[4096,8]{0,1:T(8,128)(2,1)S(1)} %collective-permute-done.1), channel_id=1, source_target_pairs={{0,1},{1,2},{2,3},{3,4},{4,5},{5,6},{6,7},{7,0},{8,9},{9,10},{10,1... | collective-permute-start | bytes 196616 | tf_op jit(solution)/shard_map/ppermute | solution.py:21
  31.1 23.8 %collective-permute-start.3 = (bf16[4096,8]{0,1:T(8,128)(2,1)S(1)}, bf16[4096,8]{0,1:T(8,128)(2,1)S(1)}, u32[]{:S(2)}, u32[]{:S(2)}) collective-permute-start(bf16[4096,8]{0,1:T(8,128)(2,1)S(1)} %collective-permute-done.2), channel_id=1, source_target_pairs={{0,1},{1,2},{2,3},{3,4},{4,5},{5,6},{6,7},{7,0},{8,9},{9,10},{10,1... | collective-permute-start | bytes 196616 | tf_op jit(solution)/shard_map/ppermute | solution.py:21
  54.8 7.0 %collective-permute-start.4 = (bf16[4096,8]{0,1:T(8,128)(2,1)S(1)}, bf16[4096,8]{0,1:T(8,128)(2,1)S(1)}, u32[]{:S(2)}, u32[]{:S(2)}) collective-permute-start(bf16[4096,8]{0,1:T(8,128)(2,1)S(1)} %collective-permute-done.3), channel_id=1, source_target_pairs={{0,1},{1,2},{2,3},{3,4},{4,5},{5,6},{6,7},{7,0},{8,9},{9,10},{10,1... | collective-permute-start | bytes 196616 | tf_op jit(solution)/shard_map/ppermute | solution.py:21
  61.9 7.3 %collective-permute-start.5 = (bf16[4096,8]{0,1:T(8,128)(2,1)S(1)}, bf16[4096,8]{0,1:T(8,128)(2,1)S(1)}, u32[]{:S(2)}, u32[]{:S(2)}) collective-permute-start(bf16[4096,8]{0,1:T(8,128)(2,1)S(1)} %collective-permute-done.4), channel_id=1, source_target_pairs={{0,1},{1,2},{2,3},{3,4},{4,5},{5,6},{6,7},{7,0},{8,9},{9,10},{10,1... | collective-permute-start | bytes 196616 | tf_op jit(solution)/shard_map/ppermute | solution.py:21
  69.2 19.3 %collective-permute-start.6 = (bf16[4096,8]{0,1:T(8,128)(2,1)S(1)}, bf16[4096,8]{0,1:T(8,128)(2,1)S(1)}, u32[]{:S(2)}, u32[]{:S(2)}) collective-permute-start(bf16[4096,8]{0,1:T(8,128)(2,1)S(1)} %collective-permute-done.5), channel_id=1, source_target_pairs={{0,1},{1,2},{2,3},{3,4},{4,5},{5,6},{6,7},{7,0},{8,9},{9,10},{10,1... | collective-permute-start | bytes 196616 | tf_op jit(solution)/shard_map/ppermute | solution.py:21
Sparse Core Ops, SparseCore 0:
  110.3 22.1 all-reduce.2
